TPU v7x, 32 devices: a whole 2x2x4 slice. The times are simulated.
32 devices in a mesh: dp: 8 (over z, x), tensor: 4 (over y, core).
Axes of the slice: x: 2, y: 2, z: 4, core: 2. Of those that a mesh axis runs over, the one named last changes fastest.
Arguments:
- activations: bfloat16 [16, 128, 4096], P('dp'), may hold values from -6 to 6
- out_grads: bfloat16 [16, 128, 20480], P('dp', None, 'tensor'), may hold values from -0.875 to 0.875
- act_scale: bfloat16 [16, 32], P('dp'), may hold values from 1 to 16
- grad_scale: bfloat16 [16, 1, 20480], P('dp', None, 'tensor'), may hold values from 1 to 72
- moment: float32 [20480, 4096], P(('tensor', 'dp')), may hold values from -0.6 to 0.6
- second: float32 [20480, 4096], P(('tensor', 'dp')), may hold values from 0.1 to 1
- master: float32 [20480, 4096], P(('tensor', 'dp')), may hold values from -0.0625 to 0.0625
Outputs:
- new_moment: float32 [20480, 4096], P(('tensor', 'dp'))
- new_second: float32 [20480, 4096], P(('tensor', 'dp'))
- new_master: float32 [20480, 4096], P(('tensor', 'dp'))
- weights: bfloat16 [20480, 4096], P(('tensor', 'dp'))
All inputs are finite; a program needn't handle non-finite values.
Results may differ from a plain program's by a relative error of at most 0.015.
Values may be sent and summed in bfloat16 or wider, within the bound.
A program may use at most 192 MiB of HBM per device.

v0:
```python
import jax
import jax.numpy as jnp
from jax import lax
from jax.sharding import PartitionSpec as P

FF = 20480
ROWS = 4096
TILE = 128
clip_rms = 1.0
beta_first = 0.9
beta_second = 0.95
learn_rate = 0.003
adam_eps = 1e-08


def widen(act_scale):
    tiles = act_scale.astype(jnp.float32)
    spread = jnp.broadcast_to(tiles[:, :, None], tiles.shape + (TILE,))
    return spread.reshape(tiles.shape[0], tiles.shape[1] * TILE)


def transposed_product(grads_rows, acts_rows):
    return lax.dot_general(
        grads_rows, acts_rows, (((0,), (0,)), ((), ())), preferred_element_type=jnp.float32
    )


def per_device(activations, out_grads, act_scale, grad_scale, moment, second, master):
    owners = lax.axis_size("dp")
    owned = out_grads.shape[2] // owners
    weight_rows = activations.shape[2]
    local_tokens = activations.shape[0] * activations.shape[1]
    acts_deq = (
        (activations.astype(jnp.float32) * widen(act_scale)[:, None, :])
        .astype(jnp.bfloat16)
        .reshape(local_tokens, weight_rows)
    )
    grads_deq = (
        (out_grads.astype(jnp.float32) * grad_scale.astype(jnp.float32))
        .astype(jnp.bfloat16)
        .reshape(local_tokens, out_grads.shape[2])
    )
    moved = lax.all_to_all(grads_deq, "dp", split_axis=1, concat_axis=0, tiled=True)
    piece = lax.all_gather(acts_deq, "dp", axis=0, tiled=True)
    count = piece.shape[0]

    def add_group(group, total):
        offset = (group * local_tokens).astype(jnp.int32)
        acts_group = lax.dynamic_slice_in_dim(piece, offset, local_tokens, 0)
        grads_group = lax.dynamic_slice_in_dim(moved, offset, local_tokens, 0)
        term = transposed_product(grads_group, acts_group)
        rounded = lax.optimization_barrier(term.astype(jnp.bfloat16))
        return total + rounded.astype(jnp.float32)

    grad_owned = lax.fori_loop(
        0, count // local_tokens, add_group, jnp.zeros((owned, weight_rows), jnp.float32)
    )
    squares = lax.psum(jnp.sum(grad_owned * grad_owned), ("dp", "tensor"))
    limit = clip_rms * jnp.sqrt(jnp.float32(FF * ROWS))
    factor = jnp.minimum(1.0, limit / jnp.sqrt(squares))
    clipped = factor * grad_owned
    new_moment = beta_first * moment + (1.0 - beta_first) * clipped
    new_second = beta_second * second + (1.0 - beta_second) * clipped * clipped
    new_master = master - learn_rate * new_moment / (jnp.sqrt(new_second) + adam_eps)
    weights = new_master.astype(jnp.bfloat16)
    return (new_moment, new_second, new_master, weights)


def solution(mesh):
    return jax.shard_map(
        per_device,
        mesh=mesh,
        in_specs=(
            P("dp", None, None),
            P("dp", None, "tensor"),
            P("dp", None),
            P("dp", None, "tensor"),
            P(("tensor", "dp"), None),
            P(("tensor", "dp"), None),
            P(("tensor", "dp"), None),
        ),
        out_specs=(
            P(("tensor", "dp"), None),
            P(("tensor", "dp"), None),
            P(("tensor", "dp"), None),
            P(("tensor", "dp"), None),
        ),
        check_vma=False,
    )
```

profile of v0, /device:TPU:0, one launch (start us, length us, event | category | flops | bytes accessed | tf_op | source)
XLA Modules:
  0.0 516.6 jit_solution(14019932499861952802)
XLA Ops:
  7.2 0.0 all-gather.2.cloned.1.call-start
  7.2 0.7 convert_element_type.36
  7.9 0.1 broadcast_bitcast_fusion
  8.0 3.4 multiply_convert_fusion.1
  11.4 0.0 all-gather.2.cloned.1.call-update
  11.4 0.7 bitcast_convert_fusion
  12.1 2.3 multiply_convert_fusion
  14.5 0.5 copy.12
  15.0 1.8 copy.11
  16.8 7.3 %all-to-all-start = ((bf16[256,8,640]{2,0,1:T(8,128)(2,1)}), bf16[256,8,640]{2,0,1:T(8,128)(2,1)S(1)}, u32[]{:S(2)}, u32[]{:S(2)}) async-start(bf16[256,8,640]{2,0,1:T(8,128)(2,1)} %copy.11), calls=%async_computation | async-start | bytes 5242880 | tf_op jit(solution)/shard_map/all_to_all | solution.py:43
  24.1 121.2 %all-to-all-done = bf16[256,8,640]{2,0,1:T(8,128)(2,1)S(1)} async-done(((bf16[256,8,640]{2,0,1:T(8,128)(2,1)}), bf16[256,8,640]{2,0,1:T(8,128)(2,1)S(1)}, u32[]{:S(2)}, u32[]{:S(2)}) %all-to-all-start) | async-done | bytes 2621472 | tf_op jit(solution)/shard_map/all_to_all | solution.py:43
  145.3 151.2 %all-gather.2.cloned.1.call-done = bf16[2048,4096]{1,0:T(8,128)(2,1)} async-done(((bf16[256,4096]{1,0:T(8,128)(2,1)}), bf16[2048,4096]{1,0:T(8,128)(2,1)}) %all-gather.2.cloned.1.call-update) | async-done | bytes 16777232 | tf_op jit(solution)/shard_map/all_gather | solution.py:44
  296.5 137.7 %while.14 = (s32[]{:T(128)}, f32[640,4096]{1,0:T(8,128)}, bf16[2048,640]{1,0:T(8,128)(2,1)S(1)}, bf16[2048,4096]{1,0:T(8,128)(2,1)}, s32[]{:T(128)}, /*index=5*/s32[]{:T(128)}, s32[]{:T(128)}, s32[]{:T(128)}) while((s32[]{:T(128)}, f32[640,4096]{1,0:T(8,128)}, bf16[2048,640]{1,0:T(8,128)(2,1)S(1)}, bf16[2048,4096]{1,0:T(8,128)(2,1)}, ...), condition=%wide.region_1.0_spmd.clone, body=%wide.region_0.0_spmd.clone.sunk | while | flops 1352663040 | bytes 33883284 | solution.py:55
  296.5 5.5 %convolution_convert_fusion.2 = bf16[640,4096]{1,0:T(8,128)(2,1)} fusion(bf16[2048,4096]{1,0:T(8,128)(2,1)} %get-tuple-element.155, s32[]{:T(128)S(6)} %select_n.10, bf16[2048,640]{1,0:T(8,128)(2,1)S(1)} %get-tuple-element.154), kind=kOutput, calls=%fused_computation.1.clone.1 | convolution fusion | flops 1344798720 | bytes 7668736 | tf_op jit(solution)/shard_map/while/body/eval_jaxpr/dot_general | solution.py:23
  302.0 9.1 %select_add_fusion.2 = f32[640,4096]{1,0:T(8,128)} fusion(f32[640,4096]{1,0:T(8,128)} %get-tuple-element.145, bf16[640,4096]{1,0:T(8,128)(2,1)} %convolution_convert_fusion.2, pred[]{:T(512)S(6)} %compare.3), kind=kLoop, calls=%fused_computation.clone.1 | loop fusion | flops 7864320 | bytes 26214400 | tf_op jit(solution)/shard_map/while/body/eval_jaxpr/add | solution.py:53
  311.1 5.5 %convolution_convert_fusion.2 = bf16[640,4096]{1,0:T(8,128)(2,1)} fusion(bf16[2048,4096]{1,0:T(8,128)(2,1)} %get-tuple-element.155, s32[]{:T(128)S(6)} %select_n.10, bf16[2048,640]{1,0:T(8,128)(2,1)S(1)} %get-tuple-element.154), kind=kOutput, calls=%fused_computation.1.clone.1 | convolution fusion | flops 1344798720 | bytes 7668736 | tf_op jit(solution)/shard_map/while/body/eval_jaxpr/dot_general | solution.py:23
  316.6 12.1 %select_add_fusion.2 = f32[640,4096]{1,0:T(8,128)} fusion(f32[640,4096]{1,0:T(8,128)} %get-tuple-element.145, bf16[640,4096]{1,0:T(8,128)(2,1)} %convolution_convert_fusion.2, pred[]{:T(512)S(6)} %compare.3), kind=kLoop, calls=%fused_computation.clone.1 | loop fusion | flops 7864320 | bytes 26214400 | tf_op jit(solution)/shard_map/while/body/eval_jaxpr/add | solution.py:53
  328.7 5.5 %convolution_convert_fusion.2 = bf16[640,4096]{1,0:T(8,128)(2,1)} fusion(bf16[2048,4096]{1,0:T(8,128)(2,1)} %get-tuple-element.155, s32[]{:T(128)S(6)} %select_n.10, bf16[2048,640]{1,0:T(8,128)(2,1)S(1)} %get-tuple-element.154), kind=kOutput, calls=%fused_computation.1.clone.1 | convolution fusion | flops 1344798720 | bytes 7668736 | tf_op jit(solution)/shard_map/while/body/eval_jaxpr/dot_general | solution.py:23
  334.2 12.1 %select_add_fusion.2 = f32[640,4096]{1,0:T(8,128)} fusion(f32[640,4096]{1,0:T(8,128)} %get-tuple-element.145, bf16[640,4096]{1,0:T(8,128)(2,1)} %convolution_convert_fusion.2, pred[]{:T(512)S(6)} %compare.3), kind=kLoop, calls=%fused_computation.clone.1 | loop fusion | flops 7864320 | bytes 26214400 | tf_op jit(solution)/shard_map/while/body/eval_jaxpr/add | solution.py:53
  346.3 5.5 %convolution_convert_fusion.2 = bf16[640,4096]{1,0:T(8,128)(2,1)} fusion(bf16[2048,4096]{1,0:T(8,128)(2,1)} %get-tuple-element.155, s32[]{:T(128)S(6)} %select_n.10, bf16[2048,640]{1,0:T(8,128)(2,1)S(1)} %get-tuple-element.154), kind=kOutput, calls=%fused_computation.1.clone.1 | convolution fusion | flops 1344798720 | bytes 7668736 | tf_op jit(solution)/shard_map/while/body/eval_jaxpr/dot_general | solution.py:23
  351.8 12.1 %select_add_fusion.2 = f32[640,4096]{1,0:T(8,128)} fusion(f32[640,4096]{1,0:T(8,128)} %get-tuple-element.145, bf16[640,4096]{1,0:T(8,128)(2,1)} %convolution_convert_fusion.2, pred[]{:T(512)S(6)} %compare.3), kind=kLoop, calls=%fused_computation.clone.1 | loop fusion | flops 7864320 | bytes 26214400 | tf_op jit(solution)/shard_map/while/body/eval_jaxpr/add | solution.py:53
  363.9 5.5 %convolution_convert_fusion.2 = bf16[640,4096]{1,0:T(8,128)(2,1)} fusion(bf16[2048,4096]{1,0:T(8,128)(2,1)} %get-tuple-element.155, s32[]{:T(128)S(6)} %select_n.10, bf16[2048,640]{1,0:T(8,128)(2,1)S(1)} %get-tuple-element.154), kind=kOutput, calls=%fused_computation.1.clone.1 | convolution fusion | flops 1344798720 | bytes 7668736 | tf_op jit(solution)/shard_map/while/body/eval_jaxpr/dot_general | solution.py:23
  369.4 12.1 %select_add_fusion.2 = f32[640,4096]{1,0:T(8,128)} fusion(f32[640,4096]{1,0:T(8,128)} %get-tuple-element.145, bf16[640,4096]{1,0:T(8,128)(2,1)} %convolution_convert_fusion.2, pred[]{:T(512)S(6)} %compare.3), kind=kLoop, calls=%fused_computation.clone.1 | loop fusion | flops 7864320 | bytes 26214400 | tf_op jit(solution)/shard_map/while/body/eval_jaxpr/add | solution.py:53
  381.5 5.5 %convolution_convert_fusion.2 = bf16[640,4096]{1,0:T(8,128)(2,1)} fusion(bf16[2048,4096]{1,0:T(8,128)(2,1)} %get-tuple-element.155, s32[]{:T(128)S(6)} %select_n.10, bf16[2048,640]{1,0:T(8,128)(2,1)S(1)} %get-tuple-element.154), kind=kOutput, calls=%fused_computation.1.clone.1 | convolution fusion | flops 1344798720 | bytes 7668736 | tf_op jit(solution)/shard_map/while/body/eval_jaxpr/dot_general | solution.py:23
  387.0 12.1 %select_add_fusion.2 = f32[640,4096]{1,0:T(8,128)} fusion(f32[640,4096]{1,0:T(8,128)} %get-tuple-element.145, bf16[640,4096]{1,0:T(8,128)(2,1)} %convolution_convert_fusion.2, pred[]{:T(512)S(6)} %compare.3), kind=kLoop, calls=%fused_computation.clone.1 | loop fusion | flops 7864320 | bytes 26214400 | tf_op jit(solution)/shard_map/while/body/eval_jaxpr/add | solution.py:53
  399.1 5.5 %convolution_convert_fusion.2 = bf16[640,4096]{1,0:T(8,128)(2,1)} fusion(bf16[2048,4096]{1,0:T(8,128)(2,1)} %get-tuple-element.155, s32[]{:T(128)S(6)} %select_n.10, bf16[2048,640]{1,0:T(8,128)(2,1)S(1)} %get-tuple-element.154), kind=kOutput, calls=%fused_computation.1.clone.1 | convolution fusion | flops 1344798720 | bytes 7668736 | tf_op jit(solution)/shard_map/while/body/eval_jaxpr/dot_general | solution.py:23
  404.6 12.1 %select_add_fusion.2 = f32[640,4096]{1,0:T(8,128)} fusion(f32[640,4096]{1,0:T(8,128)} %get-tuple-element.145, bf16[640,4096]{1,0:T(8,128)(2,1)} %convolution_convert_fusion.2, pred[]{:T(512)S(6)} %compare.3), kind=kLoop, calls=%fused_computation.clone.1 | loop fusion | flops 7864320 | bytes 26214400 | tf_op jit(solution)/shard_map/while/body/eval_jaxpr/add | solution.py:53
  416.7 5.5 %convolution_convert_fusion.2 = bf16[640,4096]{1,0:T(8,128)(2,1)} fusion(bf16[2048,4096]{1,0:T(8,128)(2,1)} %get-tuple-element.155, s32[]{:T(128)S(6)} %select_n.10, bf16[2048,640]{1,0:T(8,128)(2,1)S(1)} %get-tuple-element.154), kind=kOutput, calls=%fused_computation.1.clone.1 | convolution fusion | flops 1344798720 | bytes 7668736 | tf_op jit(solution)/shard_map/while/body/eval_jaxpr/dot_general | solution.py:23
  422.2 12.1 %select_add_fusion.2 = f32[640,4096]{1,0:T(8,128)} fusion(f32[640,4096]{1,0:T(8,128)} %get-tuple-element.145, bf16[640,4096]{1,0:T(8,128)(2,1)} %convolution_convert_fusion.2, pred[]{:T(512)S(6)} %compare.3), kind=kLoop, calls=%fused_computation.clone.1 | loop fusion | flops 7864320 | bytes 26214400 | tf_op jit(solution)/shard_map/while/body/eval_jaxpr/add | solution.py:53
  434.2 7.3 %multiply_reduce_fusion = f32[]{:T(128)} fusion(f32[640,4096]{1,0:T(8,128)} %get-tuple-element.83), kind=kLoop, calls=%fused_computation.9 | loop fusion | flops 5242879 | bytes 10485764 | tf_op jit(solution)/shard_map/reduce_sum | solution.py:58
  441.5 38.6 %psum.7 = f32[]{:T(128)} all-reduce(f32[]{:T(128)} %multiply_reduce_fusion), channel_id=1, replica_groups=mesh['dp'=8,'tensor'=4] {'dp','tensor'}, use_global_device_ids=true, to_apply=%region_3.0 | all-reduce | flops 1 | bytes 8 | tf_op jit(solution)/shard_map/psum | solution.py:58
  480.8 28.9 %fusion.4 = (bf16[640,4096]{1,0:T(8,128)(2,1)}, f32[640,4096]{1,0:T(8,128)}, f32[640,4096]{1,0:T(8,128)}, f32[640,4096]{1,0:T(8,128)}) fusion(f32[640,4096]{1,0:T(8,128)} %param.15, f32[640,4096]{1,0:T(8,128)} %get-tuple-element.83, f32[]{:T(128)S(6)} %min.3, f32[640,4096]{1,0:T(8,128)} %param.14, f32[640,4096]{1,0:T(8,128)} %param.13), kind=kLoop, calls=%fused_computation.15 | loop fusion | flops 34078720 | bytes 78643200 | tf_op jit(solution)/shard_map/convert_element_type | solution.py:65
  (2 shorter events, 0.0 us)
Async XLA Ops:
  7.2 289.4 %all-gather.2.cloned.1.call-start = ((), (), s32[]{:S(2)}) async-start(), calls=%async_computation.1 | async-start | bytes 18874368 | tf_op jit(solution)/shard_map/all_gather | solution.py:44
  16.8 128.5 %all-to-all-start = ((bf16[256,8,640]{2,0,1:T(8,128)(2,1)}), bf16[256,8,640]{2,0,1:T(8,128)(2,1)S(1)}, u32[]{:S(2)}, u32[]{:S(2)}) async-start(bf16[256,8,640]{2,0,1:T(8,128)(2,1)} %copy.11), calls=%async_computation | async-start | bytes 5242880 | tf_op jit(solution)/shard_map/all_to_all | solution.py:43
Sparse Core Ops, SparseCore 0:
  11.5 284.9 all-gather.1
where the time goes:
time: 517 us
  waiting for transfers between devices  272 us (53%)
  other arithmetic  137 us (26%)
  matrix products  44 us (9%)
  blocking collectives  38.6 us (7%)
  between operations  14.8 us (3%)
  starting transfers between devices  7.32 us (1%)
    all_gather x1, waiting for transfers between devices, per_device(): piece = lax.all_gather(acts_deq, 'dp', axis=0, tiled=True)  151 us
    all_to_all x1, waiting for transfers between devices, per_device(): lax.all_to_all(grads_deq, 'dp', split_axis=1, concat_axis=0, tiled=True)  121 us
    add x8, other arithmetic, add_group(): return total + rounded.astype(jnp.float32)  93.7 us
    dot_general x8, matrix products, transposed_product(): lax.dot_general(grads_rows, acts_rows, (((0,), (0,)), ((), ())), preferre...  44 us
    psum x1, blocking collectives, per_device(): squares = lax.psum(jnp.sum(grad_owned * grad_owned), ('dp', 'tensor'))  38.6 us
    convert_element_type x1, other arithmetic, per_device(): weights = new_master.astype(jnp.bfloat16)  28.9 us
  transfers between devices with their start and end apart: 2, of which 2 were waited for; matrix products, arithmetic and copies ran while one was open for 1% of the time, Pallas kernels for 0%

commit v1 on v0

--- a/solution.py
+++ b/solution.py
@@ -41,7 +41,18 @@
         .reshape(local_tokens, out_grads.shape[2])
     )
     moved = lax.all_to_all(grads_deq, "dp", split_axis=1, concat_axis=0, tiled=True)
-    piece = lax.all_gather(acts_deq, "dp", axis=0, tiled=True)
+    n_blocks = lax.axis_size("dp")
+    val = sorted(((no, (no + 1) % n_blocks) for no in range(n_blocks)))
+    carry_out = acts_deq
+    heap = [carry_out]
+    i0 = 1
+    while i0 < n_blocks:
+        carry_out = lax.ppermute(carry_out, axis_name="dp", perm=val)
+        heap.insert(0, carry_out)
+        i0 += 1
+    q_next = jnp.concatenate(heap, axis=0)
+    high = lax.axis_index("dp") + 1
+    piece = jnp.roll(q_next, high * acts_deq.shape[0], axis=0)
     count = piece.shape[0]
 
     def add_group(group, total):

time: 517 us -> 616 us (1.19)
  waiting for transfers between devices: 272 us -> 341 us
  local copies, waits for them, and re-layouts: 2.41 us -> 28.1 us
  blocking collectives: 38.6 us -> 53.5 us
  between operations: 14.8 us -> 1.56 us
    ppermute x0 -> x7, waiting for transfers between devices: none -> 341 us  [per_device(): carry_out = lax.ppermute(carry_out, axis_name='dp', perm=val)]
    all_gather x1 -> x0, waiting for transfers between devices: 151 us -> none  [per_device(): piece = lax.all_gather(acts_deq, 'dp', axis=0, tiled=True)]
    all_to_all x1, waiting for transfers between devices: 121 us -> 0.01 us  [per_device(): lax.all_to_all(grads_deq, 'dp', split_axis=1, concat_axis=0, tiled=True)]
    unnamed x3 -> x36, local copies, waits for them, and re-layouts: 0.59 us -> 19.6 us
    psum x1, blocking collectives: 38.6 us -> 53.5 us  [per_device(): squares = lax.psum(jnp.sum(grad_owned * grad_owned), ('dp', 'tensor'))]
    dynamic_slice x0 -> x1, local copies, waits for them, and re-layouts: none -> 6.55 us  [per_device(): piece = jnp.roll(q_next, high * acts_deq.shape[0], axis=0)]
  transfers between devices with their start and end apart: 2 -> 8, of which waited for: 2 -> 7; matrix products, arithmetic and copies ran while one was open for 1% -> 4% of each run, Pallas kernels for 0% -> 0%
where the time goes in v1:
time: 616 us; the launch traced here: 614 us
  waiting for transfers between devices  341 us (55%)
  other arithmetic  136 us (22%)
  blocking collectives  53.5 us (9%)
  matrix products  45 us (7%)
  local copies, waits for them, and re-layouts  28.1 us (5%)
  starting transfers between devices  9.03 us (1%)
    ppermute x7, waiting for transfers between devices, per_device(): carry_out = lax.ppermute(carry_out, axis_name='dp', perm=val)  341 us
    add x8, other arithmetic, add_group(): return total + rounded.astype(jnp.float32)  93.7 us
    psum x1, blocking collectives, per_device(): squares = lax.psum(jnp.sum(grad_owned * grad_owned), ('dp', 'tensor'))  53.5 us
    dot_general x8, matrix products, transposed_product(): lax.dot_general(grads_rows, acts_rows, (((0,), (0,)), ((), ())), preferre...  45 us
    convert_element_type x1, other arithmetic, per_device(): weights = new_master.astype(jnp.bfloat16)  28.9 us
    unnamed x36, local copies, waits for them, and re-layouts  19.6 us
  transfers between devices with their start and end apart: 8, of which 7 were waited for; matrix products, arithmetic and copies ran while one was open for 4% of the time, Pallas kernels for 0%

profile of v1, /device:TPU:0, one launch (start us, length us, event | category | flops | bytes accessed | tf_op | source)
XLA Modules:
  0.0 614.3 jit_solution(12160294107542235938)
XLA Ops:
  0.6 0.7 convert_element_type.36
  1.4 2.1 multiply_convert_fusion.1
  3.5 3.0 collective-permute-start
  6.5 48.7 %collective-permute-done = bf16[256,4096]{1,0:T(8,128)(2,1)S(1)} collective-permute-done((bf16[256,4096]{1,0:T(8,128)(2,1)S(1)}, bf16[256,4096]{1,0:T(8,128)(2,1)S(1)}, u32[]{:S(2)}, u32[]{:S(2)}) %collective-permute-start) | collective-permute-done | bytes 2097184 | tf_op jit(solution)/shard_map/ppermute | solution.py:50
  55.1 1.3 copy-done
  56.5 49.5 %collective-permute-done.1 = bf16[256,4096]{1,0:T(8,128)(2,1)S(1)} collective-permute-done((bf16[256,4096]{1,0:T(8,128)(2,1)S(1)}, bf16[256,4096]{1,0:T(8,128)(2,1)S(1)}, u32[]{:S(2)}, u32[]{:S(2)}) %collective-permute-start.1) | collective-permute-done | bytes 2097184 | tf_op jit(solution)/shard_map/ppermute | solution.py:50
  106.0 1.3 copy-done.2
  107.3 48.6 %collective-permute-done.2 = bf16[256,4096]{1,0:T(8,128)(2,1)S(1)} collective-permute-done((bf16[256,4096]{1,0:T(8,128)(2,1)S(1)}, bf16[256,4096]{1,0:T(8,128)(2,1)S(1)}, u32[]{:S(2)}, u32[]{:S(2)}) %collective-permute-start.2) | collective-permute-done | bytes 2097184 | tf_op jit(solution)/shard_map/ppermute | solution.py:50
  156.0 1.4 copy-done.4
  157.3 47.8 %collective-permute-done.3 = bf16[256,4096]{1,0:T(8,128)(2,1)S(1)} collective-permute-done((bf16[256,4096]{1,0:T(8,128)(2,1)S(1)}, bf16[256,4096]{1,0:T(8,128)(2,1)S(1)}, u32[]{:S(2)}, u32[]{:S(2)}) %collective-permute-start.3) | collective-permute-done | bytes 2097184 | tf_op jit(solution)/shard_map/ppermute | solution.py:50
  205.1 1.3 copy-done.6
  206.4 46.9 %collective-permute-done.4 = bf16[256,4096]{1,0:T(8,128)(2,1)S(1)} collective-permute-done((bf16[256,4096]{1,0:T(8,128)(2,1)S(1)}, bf16[256,4096]{1,0:T(8,128)(2,1)S(1)}, u32[]{:S(2)}, u32[]{:S(2)}) %collective-permute-start.4) | collective-permute-done | bytes 2097184 | tf_op jit(solution)/shard_map/ppermute | solution.py:50
  253.4 1.3 copy-done.8
  254.7 46.2 %collective-permute-done.5 = bf16[256,4096]{1,0:T(8,128)(2,1)} collective-permute-done((bf16[256,4096]{1,0:T(8,128)(2,1)S(1)}, bf16[256,4096]{1,0:T(8,128)(2,1)}, u32[]{:S(2)}, u32[]{:S(2)}) %collective-permute-start.5) | collective-permute-done | bytes 2097184 | tf_op jit(solution)/shard_map/ppermute | solution.py:50
  300.8 0.7 bitcast_convert_fusion
  301.6 2.3 multiply_convert_fusion
  303.9 0.5 copy.12
  304.4 1.8 copy.11
  306.2 6.0 all-to-all-start
  312.3 53.8 %collective-permute-done.6 = bf16[256,4096]{1,0:T(8,128)(2,1)} collective-permute-done((bf16[256,4096]{1,0:T(8,128)(2,1)}, bf16[256,4096]{1,0:T(8,128)(2,1)}, u32[]{:S(2)}, u32[]{:S(2)}) %collective-permute-start.6) | collective-permute-done | bytes 2097184 | tf_op jit(solution)/shard_map/ppermute | solution.py:50
  366.1 1.7 constant_dynamic-update-slice_fusion.15
  367.8 1.9 constant_dynamic-update-slice_fusion.14
  369.7 1.7 constant_dynamic-update-slice_fusion.13
  372.5 1.7 constant_dynamic-update-slice_fusion.7
  374.2 1.7 constant_dynamic-update-slice_fusion.6
  375.9 1.7 constant_dynamic-update-slice_fusion.5
  378.1 0.2 constant_dynamic-update-slice_fusion.2
  378.7 6.5 %constant_dynamic-slice_fusion = bf16[2048,4096]{1,0:T(8,128)(2,1)} fusion(bf16[4096,4096]{1,0:T(8,128)(2,1)S(1)} %constant_dynamic-update-slice_fusion, s32[]{:T(128)S(6)} %select_n.22), kind=kLoop, calls=%fused_computation.31 | loop fusion | bytes 33554436 | tf_op jit(solution)/shard_map/jit(_roll_dynamic)/dynamic_slice | solution.py:55
  385.3 138.7 %while.14 = (s32[]{:T(128)}, f32[640,4096]{1,0:T(8,128)}, bf16[2048,640]{1,0:T(8,128)(2,1)}, bf16[2048,4096]{1,0:T(8,128)(2,1)}, s32[]{:T(128)}, /*index=5*/s32[]{:T(128)}, s32[]{:T(128)}, s32[]{:T(128)}) while((s32[]{:T(128)}, f32[640,4096]{1,0:T(8,128)}, bf16[2048,640]{1,0:T(8,128)(2,1)}, bf16[2048,4096]{1,0:T(8,128)(2,1)}, ...), condition=%wide.region_1.2_spmd.clone, body=%wide.region_0.1_spmd.clone.sunk | while | flops 1352663040 | bytes 33883276 | solution.py:66
  385.3 5.6 convolution_convert_fusion.2
  390.9 9.1 %select_add_fusion.2 = f32[640,4096]{1,0:T(8,128)} fusion(f32[640,4096]{1,0:T(8,128)} %get-tuple-element.145, bf16[640,4096]{1,0:T(8,128)(2,1)} %convolution_convert_fusion.2, pred[]{:T(512)S(6)} %compare.4), kind=kLoop, calls=%fused_computation.clone.1 | loop fusion | flops 7864320 | bytes 26214400 | tf_op jit(solution)/shard_map/while/body/eval_jaxpr/add | solution.py:64
  400.0 5.6 convolution_convert_fusion.2
  405.6 12.1 %select_add_fusion.2 = f32[640,4096]{1,0:T(8,128)} fusion(f32[640,4096]{1,0:T(8,128)} %get-tuple-element.145, bf16[640,4096]{1,0:T(8,128)(2,1)} %convolution_convert_fusion.2, pred[]{:T(512)S(6)} %compare.4), kind=kLoop, calls=%fused_computation.clone.1 | loop fusion | flops 7864320 | bytes 26214400 | tf_op jit(solution)/shard_map/while/body/eval_jaxpr/add | solution.py:64
  417.7 5.6 convolution_convert_fusion.2
  423.3 12.1 %select_add_fusion.2 = f32[640,4096]{1,0:T(8,128)} fusion(f32[640,4096]{1,0:T(8,128)} %get-tuple-element.145, bf16[640,4096]{1,0:T(8,128)(2,1)} %convolution_convert_fusion.2, pred[]{:T(512)S(6)} %compare.4), kind=kLoop, calls=%fused_computation.clone.1 | loop fusion | flops 7864320 | bytes 26214400 | tf_op jit(solution)/shard_map/while/body/eval_jaxpr/add | solution.py:64
  435.4 5.6 convolution_convert_fusion.2
  441.0 12.1 %select_add_fusion.2 = f32[640,4096]{1,0:T(8,128)} fusion(f32[640,4096]{1,0:T(8,128)} %get-tuple-element.145, bf16[640,4096]{1,0:T(8,128)(2,1)} %convolution_convert_fusion.2, pred[]{:T(512)S(6)} %compare.4), kind=kLoop, calls=%fused_computation.clone.1 | loop fusion | flops 7864320 | bytes 26214400 | tf_op jit(solution)/shard_map/while/body/eval_jaxpr/add | solution.py:64
  453.1 5.6 convolution_convert_fusion.2
  458.7 12.1 %select_add_fusion.2 = f32[640,4096]{1,0:T(8,128)} fusion(f32[640,4096]{1,0:T(8,128)} %get-tuple-element.145, bf16[640,4096]{1,0:T(8,128)(2,1)} %convolution_convert_fusion.2, pred[]{:T(512)S(6)} %compare.4), kind=kLoop, calls=%fused_computation.clone.1 | loop fusion | flops 7864320 | bytes 26214400 | tf_op jit(solution)/shard_map/while/body/eval_jaxpr/add | solution.py:64
  470.8 5.6 convolution_convert_fusion.2
  476.4 12.1 %select_add_fusion.2 = f32[640,4096]{1,0:T(8,128)} fusion(f32[640,4096]{1,0:T(8,128)} %get-tuple-element.145, bf16[640,4096]{1,0:T(8,128)(2,1)} %convolution_convert_fusion.2, pred[]{:T(512)S(6)} %compare.4), kind=kLoop, calls=%fused_computation.clone.1 | loop fusion | flops 7864320 | bytes 26214400 | tf_op jit(solution)/shard_map/while/body/eval_jaxpr/add | solution.py:64
  488.5 5.6 convolution_convert_fusion.2
  494.1 12.1 %select_add_fusion.2 = f32[640,4096]{1,0:T(8,128)} fusion(f32[640,4096]{1,0:T(8,128)} %get-tuple-element.145, bf16[640,4096]{1,0:T(8,128)(2,1)} %convolution_convert_fusion.2, pred[]{:T(512)S(6)} %compare.4), kind=kLoop, calls=%fused_computation.clone.1 | loop fusion | flops 7864320 | bytes 26214400 | tf_op jit(solution)/shard_map/while/body/eval_jaxpr/add | solution.py:64
  506.2 5.6 convolution_convert_fusion.2
  511.8 12.1 %select_add_fusion.2 = f32[640,4096]{1,0:T(8,128)} fusion(f32[640,4096]{1,0:T(8,128)} %get-tuple-element.145, bf16[640,4096]{1,0:T(8,128)(2,1)} %convolution_convert_fusion.2, pred[]{:T(512)S(6)} %compare.4), kind=kLoop, calls=%fused_computation.clone.1 | loop fusion | flops 7864320 | bytes 26214400 | tf_op jit(solution)/shard_map/while/body/eval_jaxpr/add | solution.py:64
  523.9 7.3 %multiply_reduce_fusion = f32[]{:T(128)} fusion(f32[640,4096]{1,0:T(8,128)} %get-tuple-element.83), kind=kLoop, calls=%fused_computation.9 | loop fusion | flops 5242879 | bytes 10485764 | tf_op jit(solution)/shard_map/reduce_sum | solution.py:69
  531.2 53.5 %psum.7 = f32[]{:T(128)} all-reduce(f32[]{:T(128)} %multiply_reduce_fusion), channel_id=1, replica_groups=mesh['dp'=8,'tensor'=4] {'dp','tensor'}, use_global_device_ids=true, to_apply=%region_3.4 | all-reduce | flops 1 | bytes 8 | tf_op jit(solution)/shard_map/psum | solution.py:69
  585.4 28.9 %fusion.4 = (bf16[640,4096]{1,0:T(8,128)(2,1)}, f32[640,4096]{1,0:T(8,128)}, f32[640,4096]{1,0:T(8,128)}, f32[640,4096]{1,0:T(8,128)}) fusion(f32[640,4096]{1,0:T(8,128)} %param.15, f32[640,4096]{1,0:T(8,128)} %get-tuple-element.83, f32[]{:T(128)S(6)} %min.3, f32[640,4096]{1,0:T(8,128)} %param.14, f32[640,4096]{1,0:T(8,128)} %param.13), kind=kLoop, calls=%fused_computation.32 | loop fusion | flops 34078720 | bytes 78643200 | tf_op jit(solution)/shard_map/convert_element_type | solution.py:76
  (32 shorter events, 1.9 us)
Async XLA Ops:
  3.5 51.7 %collective-permute-start = (bf16[256,4096]{1,0:T(8,128)(2,1)S(1)}, bf16[256,4096]{1,0:T(8,128)(2,1)S(1)}, u32[]{:S(2)}, u32[]{:S(2)}) collective-permute-start(bf16[256,4096]{1,0:T(8,128)(2,1)S(1)} %bitcast.15), channel_id=1, source_target_pairs={{0,4},{4,8},{8,12},{12,16},{16,20},{20,24},{24,28},{28,0},{1,5},{5... | collective-permute-start | bytes 6291464 | tf_op jit(solution)/shard_map/ppermute | solution.py:50
  55.1 1.3 copy-start
  56.5 49.5 %collective-permute-start.1 = (bf16[256,4096]{1,0:T(8,128)(2,1)S(1)}, bf16[256,4096]{1,0:T(8,128)(2,1)S(1)}, u32[]{:S(2)}, u32[]{:S(2)}) collective-permute-start(bf16[256,4096]{1,0:T(8,128)(2,1)S(1)} %collective-permute-done), channel_id=1, source_target_pairs={{0,4},{4,8},{8,12},{12,16},{16,20},{20,24},{24,28},{28,0},{1,5},{5... | collective-permute-start | bytes 6291464 | tf_op jit(solution)/shard_map/ppermute | solution.py:50
  106.0 1.3 copy-start.2
  107.3 48.6 %collective-permute-start.2 = (bf16[256,4096]{1,0:T(8,128)(2,1)S(1)}, bf16[256,4096]{1,0:T(8,128)(2,1)S(1)}, u32[]{:S(2)}, u32[]{:S(2)}) collective-permute-start(bf16[256,4096]{1,0:T(8,128)(2,1)S(1)} %collective-permute-done.1), channel_id=1, source_target_pairs={{0,4},{4,8},{8,12},{12,16},{16,20},{20,24},{24,28},{28,0},{1,5},{5... | collective-permute-start | bytes 6291464 | tf_op jit(solution)/shard_map/ppermute | solution.py:50
  156.0 1.4 copy-start.4
  157.3 47.8 %collective-permute-start.3 = (bf16[256,4096]{1,0:T(8,128)(2,1)S(1)}, bf16[256,4096]{1,0:T(8,128)(2,1)S(1)}, u32[]{:S(2)}, u32[]{:S(2)}) collective-permute-start(bf16[256,4096]{1,0:T(8,128)(2,1)S(1)} %collective-permute-done.2), channel_id=1, source_target_pairs={{0,4},{4,8},{8,12},{12,16},{16,20},{20,24},{24,28},{28,0},{1,5},{5... | collective-permute-start | bytes 6291464 | tf_op jit(solution)/shard_map/ppermute | solution.py:50
  205.1 1.3 copy-start.6
  206.4 46.9 %collective-permute-start.4 = (bf16[256,4096]{1,0:T(8,128)(2,1)S(1)}, bf16[256,4096]{1,0:T(8,128)(2,1)S(1)}, u32[]{:S(2)}, u32[]{:S(2)}) collective-permute-start(bf16[256,4096]{1,0:T(8,128)(2,1)S(1)} %collective-permute-done.3), channel_id=1, source_target_pairs={{0,4},{4,8},{8,12},{12,16},{16,20},{20,24},{24,28},{28,0},{1,5},{5... | collective-permute-start | bytes 6291464 | tf_op jit(solution)/shard_map/ppermute | solution.py:50
  253.4 1.3 copy-start.8
  254.7 46.2 %collective-permute-start.5 = (bf16[256,4096]{1,0:T(8,128)(2,1)S(1)}, bf16[256,4096]{1,0:T(8,128)(2,1)}, u32[]{:S(2)}, u32[]{:S(2)}) collective-permute-start(bf16[256,4096]{1,0:T(8,128)(2,1)S(1)} %collective-permute-done.4), channel_id=1, source_target_pairs={{0,4},{4,8},{8,12},{12,16},{16,20},{20,24},{24,28},{28,0},{1,5},{5... | collective-permute-start | bytes 6291464 | tf_op jit(solution)/shard_map/ppermute | solution.py:50
  300.8 65.2 %collective-permute-start.6 = (bf16[256,4096]{1,0:T(8,128)(2,1)}, bf16[256,4096]{1,0:T(8,128)(2,1)}, u32[]{:S(2)}, u32[]{:S(2)}) collective-permute-start(bf16[256,4096]{1,0:T(8,128)(2,1)} %collective-permute-done.5), channel_id=1, source_target_pairs={{0,4},{4,8},{8,12},{12,16},{16,20},{20,24},{24,28},{28,0},{1,5},{5... | collective-permute-start | bytes 6291464 | tf_op jit(solution)/shard_map/ppermute | solution.py:50
  306.2 79.0 %all-to-all-start = ((bf16[256,8,640]{2,0,1:T(8,128)(2,1)}), bf16[256,8,640]{2,0,1:T(8,128)(2,1)}, u32[]{:S(2)}, u32[]{:S(2)}) async-start(bf16[256,8,640]{2,0,1:T(8,128)(2,1)} %copy.11), calls=%async_computation | async-start | bytes 5242880 | tf_op jit(solution)/shard_map/all_to_all | solution.py:43
  312.2 59.2 %copy-start.7 = (bf16[256,4096]{1,0:T(8,128)(2,1)S(1)}, bf16[256,4096]{1,0:T(8,128)(2,1)}, u32[]{:S(2)}) copy-start(bf16[256,4096]{1,0:T(8,128)(2,1)} %copy-done.6) | copy-start | bytes 6291460
  312.2 59.4 %copy-start.5 = (bf16[256,4096]{1,0:T(8,128)(2,1)S(1)}, bf16[256,4096]{1,0:T(8,128)(2,1)}, u32[]{:S(2)}) copy-start(bf16[256,4096]{1,0:T(8,128)(2,1)} %copy-done.4) | copy-start | bytes 6291460
  312.2 59.6 %copy-start.3 = (bf16[256,4096]{1,0:T(8,128)(2,1)S(1)}, bf16[256,4096]{1,0:T(8,128)(2,1)}, u32[]{:S(2)}) copy-start(bf16[256,4096]{1,0:T(8,128)(2,1)} %copy-done.2) | copy-start | bytes 6291460
  367.8 4.3 copy-start.1
